TPU v7x, 32 devices: a whole 2x2x4 slice. The times are simulated.
32 devices in a mesh: dp: 8 (over z, x), param: 4 (over y, core).
Axes of the slice: x: 2, y: 2, z: 4, core: 2. Of those that a mesh axis runs over, the one named last changes fastest.
Arguments:
- ex_grads: bfloat16 [768, 5120], P('dp', 'param'), may hold values from -6 to 6
- tgt_grads: bfloat16 [2048, 5120], P('dp', 'param'), may hold values from -6 to 6
- projection: bfloat16 [5120, 4096], P('param'), may hold values from -0.078125 to 0.078125
- example_weight: float32 [768], P('param'), may hold values from 0.05 to 1
Outputs:
- scores: float32 [2048, 768], P('dp', 'param')
All inputs are finite; a program needn't handle non-finite values.
Results may differ from a plain program's by a relative error of at most 0.0078.
Values may be sent and summed in bfloat16 or wider, within the bound.
A program may use at most 192 MiB of HBM per device.

v0:
```python
import math
import jax
import jax.numpy as jnp
from jax import lax
from jax.sharding import PartitionSpec as P

ridge_value = 0.5


def with_ridge(block, first_row):
    row_ids = lax.broadcasted_iota(jnp.int32, block.shape, 0) + first_row
    col_ids = lax.broadcasted_iota(jnp.int32, block.shape, 1)
    return block + jnp.where(row_ids == col_ids, ridge_value, 0.0).astype(jnp.float32)


def on_device(ex_grads, tgt_grads, projection, example_weight):
    ex_rows = ex_grads.shape[0]
    columns = projection.shape[1]
    param_total = lax.axis_size("param")
    param_pos = lax.axis_index("param")
    replica_pos = lax.axis_index("dp")
    stacked = jnp.concatenate([ex_grads, tgt_grads], axis=0)
    contract_rows = (((0,), (1,)), ((), ()))
    feature_block = lax.psum_scatter(
        lax.dot_general(projection, stacked, contract_rows, preferred_element_type=jnp.float32),
        "param",
        scatter_dimension=0,
        tiled=True,
    )
    local_features = feature_block.astype(jnp.bfloat16)
    example_part = local_features[:, :ex_rows]
    contract_first = (((0,), (0,)), ((), ()))
    partial_value = lax.dot_general(
        local_features,
        lax.all_gather(example_part, "dp", axis=1, tiled=True),
        contract_first,
        preferred_element_type=jnp.float32,
    )
    examples = partial_value.shape[1]
    summed = lax.psum(partial_value, "param")
    kernel_block = with_ridge(summed[:ex_rows] / columns, replica_pos * ex_rows)
    kernel = lax.all_gather(kernel_block, "dp", axis=0, tiled=True)
    cross_terms = summed[ex_rows:] / columns
    factor = jnp.linalg.cholesky(kernel)
    forward = jax.scipy.linalg.solve_triangular(factor, cross_terms.T, lower=True)
    solved = jax.scipy.linalg.solve_triangular(factor, forward, lower=True, trans=1)
    block_cols = examples // param_total
    chosen = lax.dynamic_slice_in_dim(solved.T, param_pos * block_cols, block_cols, 1)
    return chosen * math.sqrt(columns) * example_weight[None, :]


def solution(mesh):
    placed = (P("dp", "param"), P("dp", "param"), P("param", None), P("param"))
    return jax.shard_map(
        on_device, mesh=mesh, in_specs=placed, out_specs=P("dp", "param"), check_vma=False
    )
```

profile of v0, /device:TPU:0, one launch (start us, length us, event | category | flops | bytes accessed | tf_op | source)
XLA Modules:
  0.0 462.6 jit_solution(8862410163447170017)
XLA Ops:
  6.5 10.7 %convolution_bitcast_fusion = f32[4096,352]{0,1:T(8,128)} fusion(bf16[1280,4096]{1,0:T(8,128)(2,1)} %param.6, bf16[256,1280]{1,0:T(8,128)(2,1)} %param.5, bf16[96,1280]{1,0:T(8,128)(2,1)} %param.4), kind=kOutput, calls=%fused_computation.2 | convolution fusion | flops 3692789760 | bytes 17154048 | tf_op jit(solution)/shard_map/dot_general | solution.py:25
  17.3 57.3 %reduce-scatter.2.cloned.1.call-done = f32[1024,352]{0,1:T(8,128)} async-done(((f32[4096,352]{0,1:T(8,128)}), f32[1024,352]{0,1:T(8,128)}) %reduce-scatter.2.cloned.1.call-update) | async-done | bytes 1441808 | tf_op jit(solution)/shard_map/reduce_scatter | solution.py:24
  74.6 1.5 convert_element_type.3
  76.1 0.7 slice.254
  76.9 44.3 %all-gather.3.cloned.1.call-done = bf16[1024,768]{0,1:T(8,128)(2,1)} async-done(((bf16[1024,96]{0,1:T(8,128)(2,1)}), bf16[1024,768]{0,1:T(8,128)(2,1)}) %all-gather.3.cloned.1.call-update) | async-done | bytes 1572880 | tf_op jit(solution)/shard_map/all_gather | solution.py:35
  121.2 3.2 fusion.85
  124.4 35.1 %all-reduce.3.cloned.1.call-done = f32[352,768]{1,0:T(8,128)} async-done(((f32[352,768]{1,0:T(8,128)}), f32[352,768]{1,0:T(8,128)}) %all-reduce.3.cloned.1.call-update) | async-done | bytes 1081360 | tf_op jit(solution)/shard_map/psum | solution.py:40
  159.6 1.8 fusion.37
  162.0 1.2 fusion.4
  163.2 50.6 %all-gather.5.cloned.1.call-done = f32[768,768]{1,0:T(8,128)} async-done(((f32[96,768]{1,0:T(8,128)}), f32[768,768]{1,0:T(8,128)}) %all-gather.5.cloned.1.call-update) | async-done | bytes 2359312 | tf_op jit(solution)/shard_map/all_gather | solution.py:42
  213.8 3.3 copy.7
  217.1 2.0 fusion
  219.1 1.4 copy-done.2
  220.5 11.7 %cholesky.165 = f32[128,128]{1,0:T(8,128)S(1)} custom-call(f32[128,128]{1,0:T(8,128)S(1)} %cholesky.424), custom_call_target="Cholesky" | custom-call | tf_op jit(solution)/shard_map/jit(cholesky)/cholesky | solution.py:44
  232.4 9.8 %custom-call.50 = f32[1,128,128]{1,2,0:T(8,128)S(1)} custom-call(f32[1,128,128]{2,1,0:T(8,128)S(1)} %get-tuple-element.38), custom_call_target="InvertDiagBlocksLowerTriangular" | custom-call | tf_op jit(solution)/shard_map/jit(cholesky)/cholesky | solution.py:44
  242.2 1.4 constant_dynamic-update-slice_fusion.20
  243.6 1.4 convolution_subtract_fusion
  245.7 12.5 %cholesky.188 = f32[128,128]{1,0:T(8,128)S(1)} custom-call(f32[128,128]{1,0:T(8,128)} %cholesky.428), custom_call_target="Cholesky" | custom-call | tf_op jit(solution)/shard_map/jit(cholesky)/cholesky | solution.py:44
  258.9 10.8 %custom-call.51 = f32[1,128,128]{1,2,0:T(8,128)S(1)} custom-call(f32[1,128,128]{2,1,0:T(8,128)} %get-tuple-element.35), custom_call_target="InvertDiagBlocksLowerTriangular" | custom-call | tf_op jit(solution)/shard_map/jit(cholesky)/cholesky | solution.py:44
  270.1 1.5 convolution_subtract_fusion.1
  271.6 11.7 %cholesky.354 = f32[128,128]{1,0:T(8,128)S(1)} custom-call(f32[128,128]{1,0:T(8,128)S(1)} %cholesky.433), custom_call_target="Cholesky" | custom-call | tf_op jit(solution)/shard_map/jit(cholesky)/cholesky | solution.py:44
  283.4 9.8 %custom-call.52 = f32[1,128,128]{1,2,0:T(8,128)S(1)} custom-call(f32[1,128,128]{2,1,0:T(8,128)S(1)} %get-tuple-element.32), custom_call_target="InvertDiagBlocksLowerTriangular" | custom-call | tf_op jit(solution)/shard_map/jit(cholesky)/cholesky | solution.py:44
  293.5 1.6 convolution_subtract_fusion.2
  295.1 12.1 %cholesky.373 = f32[128,128]{1,0:T(8,128)S(1)} custom-call(f32[128,128]{1,0:T(8,128)S(1)} %cholesky.438), custom_call_target="Cholesky" | custom-call | tf_op jit(solution)/shard_map/jit(cholesky)/cholesky | solution.py:44
  307.3 9.8 %custom-call.53 = f32[1,128,128]{1,2,0:T(8,128)S(1)} custom-call(f32[1,128,128]{2,1,0:T(8,128)S(1)} %get-tuple-element.29), custom_call_target="InvertDiagBlocksLowerTriangular" | custom-call | tf_op jit(solution)/shard_map/jit(cholesky)/cholesky | solution.py:44
  317.4 1.5 convolution_subtract_fusion.11
  318.9 11.7 %cholesky.392 = f32[128,128]{1,0:T(8,128)S(1)} custom-call(f32[128,128]{1,0:T(8,128)S(1)} %cholesky.443), custom_call_target="Cholesky" | custom-call | tf_op jit(solution)/shard_map/jit(cholesky)/cholesky | solution.py:44
  330.6 9.8 %custom-call.54 = f32[1,128,128]{1,2,0:T(8,128)S(1)} custom-call(f32[1,128,128]{2,1,0:T(8,128)S(1)} %get-tuple-element.26), custom_call_target="InvertDiagBlocksLowerTriangular" | custom-call | tf_op jit(solution)/shard_map/jit(cholesky)/cholesky | solution.py:44
  340.6 1.3 convolution_subtract_fusion.14
  342.0 11.9 %cholesky.410 = f32[128,128]{1,0:T(8,128)S(1)} custom-call(f32[128,128]{1,0:T(8,128)S(1)} %convolution_subtract_fusion.14), custom_call_target="Cholesky" | custom-call | tf_op jit(solution)/shard_map/jit(cholesky)/cholesky | solution.py:44
  353.9 0.7 compare_reduce_fusion.3
  355.9 0.7 compare_reduce_fusion
  361.0 1.6 select_select_fusion
  362.6 20.5 %while.1 = (s32[]{:T(128)}, f32[768,768]{1,0:T(8,128)}, s32[6,2]{0,1:T(2,128)S(1)}, f32[6,128,128]{2,1,0:T(8,128)}, s32[]{:T(128)}) while((s32[]{:T(128)}, f32[768,768]{1,0:T(8,128)}, s32[6,2]{0,1:T(2,128)S(1)}, f32[6,128,128]{2,1,0:T(8,128)}, s32[]{:T(128)}) %tuple.37), condition=%wide.while_cond, body=%wide.while_body.sunk | while | flops 2 | bytes 132205 | solution.py:46
  363.2 2.8 bitcast_dynamic-update-slice_fusion.2
  366.6 2.8 bitcast_dynamic-update-slice_fusion.2
  370.1 2.8 bitcast_dynamic-update-slice_fusion.2
  373.5 2.8 bitcast_dynamic-update-slice_fusion.2
  376.9 2.8 bitcast_dynamic-update-slice_fusion.2
  380.3 2.8 bitcast_dynamic-update-slice_fusion.2
  383.1 59.9 %custom-call.55 = f32[6,128,128]{1,2,0:T(8,128)S(1)} custom-call(f32[6,128,128]{2,1,0:T(8,128)} %get-tuple-element.12), custom_call_target="InvertDiagBlocksLowerTriangular" | custom-call | tf_op jit(solution)/shard_map/jit(_solve_triangular)/triangular_solve | solution.py:46
  443.3 1.2 convolution_subtract_fusion.13
  444.9 1.5 convolution_subtract_fusion.10
  446.7 0.8 convolution_subtract_fusion.9
  447.8 1.0 convolution_subtract_fusion.8
  449.2 1.3 convolution_subtract_fusion.7
  454.0 0.7 convolution_subtract_fusion.3
  455.1 0.8 multiply_bitcast_fusion
  (78 shorter events, 14.4 us)
Async XLA Ops:
  6.5 68.1 %reduce-scatter.2.cloned.1.call-start = ((), (), s32[]{:S(2)}) async-start(), calls=%async_computation.1 | async-start | bytes 7208960 | tf_op jit(solution)/shard_map/reduce_scatter | solution.py:24
  17.2 103.9 %all-gather.3.cloned.1.call-start = ((), (), s32[]{:S(2)}) async-start(), calls=%async_computation.2 | async-start | bytes 1769472 | tf_op jit(solution)/shard_map/all_gather | solution.py:35
  76.8 85.2 %copy-start.3 = (f32[192]{0:T(256)S(1)}, f32[192]{0:T(256)}, u32[]{:S(2)}) copy-start(f32[192]{0:T(256)} %param.7) | copy-start | bytes 2308
  76.8 82.7 %all-reduce.3.cloned.1.call-start = ((), (), s32[]{:S(2)}) async-start(), calls=%async_computation.3 | async-start | bytes 2162688 | tf_op jit(solution)/shard_map/psum | solution.py:40
  124.4 89.4 %all-gather.5.cloned.1.call-start = ((), (), s32[]{:S(2)}) async-start(), calls=%async_computation.4 | async-start | bytes 2654208 | tf_op jit(solution)/shard_map/all_gather | solution.py:42
  213.8 3.3 copy-start
  219.1 1.4 copy-start.2
  361.0 1.6 copy-start.4
  383.1 63.6 %copy-start.1 = (f32[768,768]{1,0:T(8,128)S(1)}, f32[768,768]{1,0:T(8,128)}, u32[]{:S(2)}) copy-start(f32[768,768]{1,0:T(8,128)} %get-tuple-element.104) | copy-start | bytes 7077892
Sparse Core Ops, SparseCore 0:
  17.4 57.2 reduce-scatter.1
  77.0 44.1 all-gather.2
  124.5 35.0 all-reduce.2
  161.6 52.1 all-gather.4
where the time goes:
time: 467 us; the launch traced here: 463 us
  other arithmetic  195 us (42%)
  waiting for transfers between devices  187 us (40%)
  matrix products  35.5 us (8%)
  local copies, waits for them, and re-layouts  26.8 us (6%)
  between operations  17.6 us (4%)
    another operation x22, other arithmetic, on_device(): factor = jnp.linalg.cholesky(kernel)  126 us
    another operation x3, other arithmetic, on_device(): jax.scipy.linalg.solve_triangular(factor, forward, lower=True, trans=1)  62.1 us
    reduce_scatter x1, waiting for transfers between devices, on_device(): lax.psum_scatter(lax.dot_general(projection, stacked, contract_rows, pref...  57.3 us
    all_gather x1, waiting for transfers between devices, on_device(): kernel = lax.all_gather(kernel_block, 'dp', axis=0, tiled=True)  50.6 us
    all_gather x1, waiting for transfers between devices, on_device(): lax.all_gather(example_part, 'dp', axis=1, tiled=True)  44.3 us
    psum x1, waiting for transfers between devices, on_device(): summed = lax.psum(partial_value, 'param')  35.1 us
    another operation x18, local copies, waits for them, and re-layouts  20.4 us
    dot_general x1, matrix products, on_device(): lax.dot_general(projection, stacked, contract_rows, preferred_element_typ...  10.7 us
  transfers between devices with their start and end apart: 4, of which 4 were waited for; matrix products, arithmetic and copies ran while one was open for 0% of the time, Pallas kernels for 0%

commit v1 on v0

--- a/solution.py
+++ b/solution.py
@@ -32,7 +32,7 @@
     contract_first = (((0,), (0,)), ((), ()))
     partial_value = lax.dot_general(
         local_features,
-        lax.all_gather(example_part, "dp", axis=1, tiled=True),
+        jnp.concatenate(lax.all_gather(example_part, "dp"), axis=1),
         contract_first,
         preferred_element_type=jnp.float32,
     )

time: 467 us -> 467 us (level)
  no operation moved by 1% of the time
where the time goes in v1:
time: 467 us; the launch traced here: 463 us
  other arithmetic  195 us (42%)
  waiting for transfers between devices  187 us (40%)
  matrix products  34.1 us (7%)
  local copies, waits for them, and re-layouts  28.4 us (6%)
  between operations  17.6 us (4%)
    another operation x22, other arithmetic, on_device(): factor = jnp.linalg.cholesky(kernel)  126 us
    another operation x3, other arithmetic, on_device(): jax.scipy.linalg.solve_triangular(factor, forward, lower=True, trans=1)  62.1 us
    reduce_scatter x1, waiting for transfers between devices, on_device(): lax.psum_scatter(lax.dot_general(projection, stacked, contract_rows, pref...  57.3 us
    all_gather x1, waiting for transfers between devices, on_device(): kernel = lax.all_gather(kernel_block, 'dp', axis=0, tiled=True)  50.6 us
    all_gather x1, waiting for transfers between devices, on_device(): lax.all_gather(example_part, 'dp')  44.3 us
    psum x1, waiting for transfers between devices, on_device(): summed = lax.psum(partial_value, 'param')  35.1 us
    another operation x18, local copies, waits for them, and re-layouts  20.4 us
    dot_general x1, matrix products, on_device(): lax.dot_general(projection, stacked, contract_rows, preferred_element_typ...  10.7 us
  transfers between devices with their start and end apart: 4, of which 4 were waited for; matrix products, arithmetic and copies ran while one was open for 0% of the time, Pallas kernels for 0%

profile of v1, /device:TPU:0, one launch (start us, length us, event | category | flops | bytes accessed | tf_op | source)
XLA Modules:
  0.0 462.8 jit_solution(10278791231557910034)
XLA Ops:
  6.5 10.7 %convolution_bitcast_fusion = f32[4096,352]{0,1:T(8,128)} fusion(bf16[1280,4096]{1,0:T(8,128)(2,1)} %param.6, bf16[256,1280]{1,0:T(8,128)(2,1)} %param.5, bf16[96,1280]{1,0:T(8,128)(2,1)} %param.4), kind=kOutput, calls=%fused_computation.2 | convolution fusion | flops 3692789760 | bytes 17154048 | tf_op jit(solution)/shard_map/dot_general | solution.py:25
  17.3 57.3 %reduce-scatter.2.cloned.1.call-done = f32[1024,352]{0,1:T(8,128)} async-done(((f32[4096,352]{0,1:T(8,128)}), f32[1024,352]{0,1:T(8,128)}) %reduce-scatter.2.cloned.1.call-update) | async-done | bytes 1441808 | tf_op jit(solution)/shard_map/reduce_scatter | solution.py:24
  74.6 1.5 convert_element_type.3
  76.9 44.3 %all-gather.6.cloned.1.call-done = bf16[8192,96]{0,1:T(8,128)(2,1)} async-done(((bf16[1024,96]{0,1:T(8,128)(2,1)}), bf16[8192,96]{0,1:T(8,128)(2,1)}) %all-gather.6.cloned.1.call-update) | async-done | bytes 1572880 | tf_op jit(solution)/shard_map/all_gather | solution.py:35
  121.2 1.5 copy.24
  122.7 1.8 fusion.85
  124.6 35.1 %all-reduce.3.cloned.1.call-done = f32[352,768]{1,0:T(8,128)} async-done(((f32[352,768]{1,0:T(8,128)}), f32[352,768]{1,0:T(8,128)}) %all-reduce.3.cloned.1.call-update) | async-done | bytes 1081360 | tf_op jit(solution)/shard_map/psum | solution.py:40
  159.7 1.8 fusion.37
  162.2 1.2 fusion.4
  163.4 50.6 %all-gather.4.cloned.1.call-done = f32[768,768]{1,0:T(8,128)} async-done(((f32[96,768]{1,0:T(8,128)}), f32[768,768]{1,0:T(8,128)}) %all-gather.4.cloned.1.call-update) | async-done | bytes 2359312 | tf_op jit(solution)/shard_map/all_gather | solution.py:42
  214.0 3.3 copy.11
  217.3 2.0 fusion
  219.3 1.4 copy-done.2
  220.7 11.7 %cholesky.165 = f32[128,128]{1,0:T(8,128)S(1)} custom-call(f32[128,128]{1,0:T(8,128)S(1)} %cholesky.424), custom_call_target="Cholesky" | custom-call | tf_op jit(solution)/shard_map/jit(cholesky)/cholesky | solution.py:44
  232.6 9.8 %custom-call.50 = f32[1,128,128]{1,2,0:T(8,128)S(1)} custom-call(f32[1,128,128]{2,1,0:T(8,128)S(1)} %get-tuple-element.38), custom_call_target="InvertDiagBlocksLowerTriangular" | custom-call | tf_op jit(solution)/shard_map/jit(cholesky)/cholesky | solution.py:44
  242.4 1.4 constant_dynamic-update-slice_fusion.20
  243.8 1.4 convolution_subtract_fusion
  245.8 12.5 %cholesky.188 = f32[128,128]{1,0:T(8,128)S(1)} custom-call(f32[128,128]{1,0:T(8,128)} %cholesky.428), custom_call_target="Cholesky" | custom-call | tf_op jit(solution)/shard_map/jit(cholesky)/cholesky | solution.py:44
  259.0 10.8 %custom-call.51 = f32[1,128,128]{1,2,0:T(8,128)S(1)} custom-call(f32[1,128,128]{2,1,0:T(8,128)} %get-tuple-element.35), custom_call_target="InvertDiagBlocksLowerTriangular" | custom-call | tf_op jit(solution)/shard_map/jit(cholesky)/cholesky | solution.py:44
  270.3 1.5 convolution_subtract_fusion.1
  271.8 11.7 %cholesky.354 = f32[128,128]{1,0:T(8,128)S(1)} custom-call(f32[128,128]{1,0:T(8,128)S(1)} %cholesky.433), custom_call_target="Cholesky" | custom-call | tf_op jit(solution)/shard_map/jit(cholesky)/cholesky | solution.py:44
  283.6 9.8 %custom-call.52 = f32[1,128,128]{1,2,0:T(8,128)S(1)} custom-call(f32[1,128,128]{2,1,0:T(8,128)S(1)} %get-tuple-element.32), custom_call_target="InvertDiagBlocksLowerTriangular" | custom-call | tf_op jit(solution)/shard_map/jit(cholesky)/cholesky | solution.py:44
  293.7 1.6 convolution_subtract_fusion.2
  295.3 12.1 %cholesky.373 = f32[128,128]{1,0:T(8,128)S(1)} custom-call(f32[128,128]{1,0:T(8,128)S(1)} %cholesky.438), custom_call_target="Cholesky" | custom-call | tf_op jit(solution)/shard_map/jit(cholesky)/cholesky | solution.py:44
  307.4 9.8 %custom-call.53 = f32[1,128,128]{1,2,0:T(8,128)S(1)} custom-call(f32[1,128,128]{2,1,0:T(8,128)S(1)} %get-tuple-element.29), custom_call_target="InvertDiagBlocksLowerTriangular" | custom-call | tf_op jit(solution)/shard_map/jit(cholesky)/cholesky | solution.py:44
  317.5 1.5 convolution_subtract_fusion.11
  319.0 11.7 %cholesky.392 = f32[128,128]{1,0:T(8,128)S(1)} custom-call(f32[128,128]{1,0:T(8,128)S(1)} %cholesky.443), custom_call_target="Cholesky" | custom-call | tf_op jit(solution)/shard_map/jit(cholesky)/cholesky | solution.py:44
  330.8 9.8 %custom-call.54 = f32[1,128,128]{1,2,0:T(8,128)S(1)} custom-call(f32[1,128,128]{2,1,0:T(8,128)S(1)} %get-tuple-element.26), custom_call_target="InvertDiagBlocksLowerTriangular" | custom-call | tf_op jit(solution)/shard_map/jit(cholesky)/cholesky | solution.py:44
  340.8 1.3 convolution_subtract_fusion.14
  342.1 11.9 %cholesky.410 = f32[128,128]{1,0:T(8,128)S(1)} custom-call(f32[128,128]{1,0:T(8,128)S(1)} %convolution_subtract_fusion.14), custom_call_target="Cholesky" | custom-call | tf_op jit(solution)/shard_map/jit(cholesky)/cholesky | solution.py:44
  354.0 0.7 compare_reduce_fusion.3
  356.0 0.7 compare_reduce_fusion
  361.2 1.6 select_select_fusion
  362.8 20.5 %while.1 = (s32[]{:T(128)}, f32[768,768]{1,0:T(8,128)}, s32[6,2]{0,1:T(2,128)S(1)}, f32[6,128,128]{2,1,0:T(8,128)}, s32[]{:T(128)}) while((s32[]{:T(128)}, f32[768,768]{1,0:T(8,128)}, s32[6,2]{0,1:T(2,128)S(1)}, f32[6,128,128]{2,1,0:T(8,128)}, s32[]{:T(128)}) %tuple.37), condition=%wide.while_cond, body=%wide.while_body.sunk | while | flops 2 | bytes 132205 | solution.py:46
  363.4 2.8 bitcast_dynamic-update-slice_fusion.2
  366.8 2.8 bitcast_dynamic-update-slice_fusion.2
  370.2 2.8 bitcast_dynamic-update-slice_fusion.2
  373.6 2.8 bitcast_dynamic-update-slice_fusion.2
  377.1 2.8 bitcast_dynamic-update-slice_fusion.2
  380.5 2.8 bitcast_dynamic-update-slice_fusion.2
  383.2 59.9 %custom-call.55 = f32[6,128,128]{1,2,0:T(8,128)S(1)} custom-call(f32[6,128,128]{2,1,0:T(8,128)} %get-tuple-element.12), custom_call_target="InvertDiagBlocksLowerTriangular" | custom-call | tf_op jit(solution)/shard_map/jit(_solve_triangular)/triangular_solve | solution.py:46
  443.5 1.2 convolution_subtract_fusion.13
  445.0 1.5 convolution_subtract_fusion.10
  446.9 0.8 convolution_subtract_fusion.9
  448.0 1.0 convolution_subtract_fusion.8
  449.4 1.3 convolution_subtract_fusion.7
  454.2 0.7 convolution_subtract_fusion.3
  455.3 0.8 multiply_bitcast_fusion
  (79 shorter events, 15.1 us)
Async XLA Ops:
  6.5 68.1 %reduce-scatter.2.cloned.1.call-start = ((), (), s32[]{:S(2)}) async-start(), calls=%async_computation.1 | async-start | bytes 7208960 | tf_op jit(solution)/shard_map/reduce_scatter | solution.py:24
  17.2 103.9 %all-gather.6.cloned.1.call-start = ((), (), s32[]{:S(2)}) async-start(), calls=%async_computation.4 | async-start | bytes 1769472 | tf_op jit(solution)/shard_map/all_gather | solution.py:35
  76.8 82.9 %all-reduce.3.cloned.1.call-start = ((), (), s32[]{:S(2)}) async-start(), calls=%async_computation.2 | async-start | bytes 2162688 | tf_op jit(solution)/shard_map/psum | solution.py:40
  122.7 39.4 %copy-start.3 = (f32[192]{0:T(256)S(1)}, f32[192]{0:T(256)}, u32[]{:S(2)}) copy-start(f32[192]{0:T(256)} %param.7) | copy-start | bytes 2308
  124.6 89.4 %all-gather.4.cloned.1.call-start = ((), (), s32[]{:S(2)}) async-start(), calls=%async_computation.3 | async-start | bytes 2654208 | tf_op jit(solution)/shard_map/all_gather | solution.py:42
  214.0 3.3 copy-start
  219.3 1.4 copy-start.2
  361.2 1.6 copy-start.4
  383.2 63.6 %copy-start.1 = (f32[768,768]{1,0:T(8,128)S(1)}, f32[768,768]{1,0:T(8,128)}, u32[]{:S(2)}) copy-start(f32[768,768]{1,0:T(8,128)} %get-tuple-element.104) | copy-start | bytes 7077892
Sparse Core Ops, SparseCore 0:
  17.4 57.2 reduce-scatter.1
  77.0 44.1 all-gather.5
  124.7 35.0 all-reduce.2
  161.8 52.1 all-gather.3
